TPU v7x, 32 devices: a whole 2x2x4 slice. The times are simulated.
32 devices in a mesh: grp: 2 (over y), lat: 16 (over z, x, core).
Axes of the slice: x: 2, y: 2, z: 4, core: 2. Of those that a mesh axis runs over, the one named last changes fastest.
Arguments:
- air_field: bfloat16 [96, 384, 1440], P(('grp', 'lat')), parts along dimension 0, may hold values from -6 to 6
- marine_field: bfloat16 [96, 200, 1440], P(('grp', 'lat')), parts along dimension 0, may hold values from -6 to 6
- water_indicator: int32 [48, 1440], P('lat'), may hold values from 0 to 1, as said below
- seam_mirror_meridian: int32 [1440], replicated, may hold values from 0 to 1439, as said below
- driving_air_latitude_index: int32 [48], P('lat'), may hold values from 0 to 46, as said below
- marine_latitude_beneath: int32 [48], P('lat'), may hold values from 0 to 47, as said below
- air_rescale_factor: float32 [384], replicated, may hold values from 0.5 to 1.5
- spectral_order_damping: float32 [48, 384], replicated, may hold values from -12 to 12
- feature_blend_matrix: bfloat16 [384, 384], replicated, may hold values from -0.3125 to 0.3125
- boundary_exchange_matrix: bfloat16 [8, 384], replicated, may hold values from -0.3125 to 0.3125
- skin_heat_response: float32 [384], replicated, may hold values from -6 to 6
- driving_feature_matrix: bfloat16 [200, 8], replicated, may hold values from -2 to 2
- planar_stencil_coefficients: float32 [9, 200], replicated, may hold values from -2 to 2
- marine_rescale_factor: float32 [200], replicated, may hold values from 0.5 to 1.5
- marine_expand_matrix: bfloat16 [800, 200], replicated, may hold values from -0.4375 to 0.4375
- marine_contract_matrix: bfloat16 [200, 800], replicated, may hold values from -0.21875 to 0.21875
Outputs:
- atmosphere_next: bfloat16 [96, 384, 1440], P(('grp', 'lat')), parts along dimension 0
- marine_field_advanced: bfloat16 [96, 200, 1440], P(('grp', 'lat')), parts along dimension 0
There are 2 independent parts, one for each index of `grp`. A program takes and returns all parts, laid end to end along the dimension named above; an argument that names none is the same for every part. Nothing has to cross between parts.
Inputs may be any that keep to these rules, and one draw needn't show every extreme that they name: `water_indicator`: among the rows of one index of lat at most 3240 cells are wet, and exactly 3240 on some index. seam_mirror_meridian[i] = (2 s - 1 - i) mod 1440 for one seam s, so it is its own inverse. Rows driving_air_latitude_index[r] and driving_air_latitude_index[r] + 1 are held by the index of lat that holds row r or by the index before it. Row marine_latitude_beneath[j] is held by the index of lat that holds row j or by the index after it.
All inputs are finite; a program needn't handle non-finite values.
Results may differ from a plain program's by a relative error of at most 0.0059.
Values may be sent and summed in bfloat16 or wider, within the bound.
A program may use at most 128 MiB of HBM per device.

v0:
```python
import math

import jax
import jax.numpy as jnp
from jax import lax
from jax.sharding import PartitionSpec as P

MMAX = 384


EPSILON = 1e-05
GELU_SCALE = 0.7978845608028654


def shifted_2(array, axis, by):
    size = lax.axis_size(axis)
    pairs = [(i, i + by) for i in range(size) if 0 <= i + by < size]
    return lax.ppermute(array, axis, pairs)


def padded_2(array, sides, width):
    for axis, dim in sides:
        size, length = (lax.axis_size(axis), array.shape[dim])
        up = [(i, (i + 1) % size) for i in range(size - 1)]
        down = [(j, i) for i, j in up]
        last = lax.slice_in_dim(array, length - width, length, axis=dim)
        leading = lax.slice_in_dim(array, 0, width, axis=dim)
        before = lax.ppermute(last, axis, up)
        after = lax.ppermute(leading, axis, down)
        array = jnp.concatenate([before, array, after], axis=dim)
    return array


def tanh_gelu(values):
    return (
        0.5 * values * (1.0 + jnp.tanh(GELU_SCALE * (values + 0.044715 * values * values * values)))
    )


def channel_norm(values, gain):
    average = jnp.mean(values, axis=-2, keepdims=True)
    centered = values - average
    variance = jnp.mean(centered * centered, axis=-2, keepdims=True)
    return centered * lax.rsqrt(variance + EPSILON) * gain[:, None]


def fourier_table(lon_count, mode_count):
    longitude = jnp.arange(lon_count, dtype=jnp.int32)
    harmonic = jnp.arange(mode_count, dtype=jnp.int32)
    phase_index = longitude[:, None] * harmonic[None, :] % lon_count
    angles = 2.0 * math.pi / lon_count * phase_index.astype(jnp.float32)
    scaled = jnp.concatenate([jnp.cos(angles), jnp.sin(angles)], axis=1) / math.sqrt(lon_count)
    return scaled.astype(jnp.bfloat16)


def latitude_table(row_count):
    row_index = jnp.arange(row_count, dtype=jnp.int32)
    phase_index = (2 * row_index[:, None] + 1) * row_index[None, :] % (4 * row_count)
    angles = math.pi / (2.0 * row_count) * phase_index.astype(jnp.float32)
    return (jnp.cos(angles) * math.sqrt(2.0 / row_count)).astype(jnp.bfloat16)


def depth_conv(extended, planar_stencil_coefficients, row_count):
    summed = jnp.zeros((row_count,) + extended.shape[1:], jnp.float32)
    for vertical in range(3):
        row_band = extended[vertical : vertical + row_count].astype(jnp.float32)
        for horizontal in range(3):
            shifted = jnp.roll(row_band, 1 - horizontal, axis=2)
            summed = (
                summed
                + planar_stencil_coefficients[3 * vertical + horizontal][None, :, None] * shifted
            )
    return summed


def spectral_filtering(gathered, lat_table, own_filter):
    spectrum = jnp.einsum("jl,jcm->lcm", lat_table, gathered, preferred_element_type=jnp.float32)
    filtered = (spectrum * own_filter[:, :, None]).astype(jnp.bfloat16)
    return jnp.einsum(
        "jl,lcm->jcm", lat_table, filtered, preferred_element_type=jnp.float32
    ).astype(jnp.bfloat16)


def local(
    air_field,
    marine_field,
    water_indicator,
    seam_mirror_meridian,
    driving_air_latitude_index,
    marine_latitude_beneath,
    air_rescale_factor,
    spectral_order_damping,
    feature_blend_matrix,
    boundary_exchange_matrix,
    skin_heat_response,
    driving_feature_matrix,
    planar_stencil_coefficients,
    marine_rescale_factor,
    marine_expand_matrix,
    marine_contract_matrix,
):
    row_count = air_field.shape[0]
    lon_count = air_field.shape[2]
    band_count = lax.axis_size("lat")
    band_index = lax.axis_index("lat")
    first_row = band_index * row_count
    atmos_float = air_field.astype(jnp.float32)
    flux = jnp.einsum(
        "fc,jcl->jfl", boundary_exchange_matrix, air_field, preferred_element_type=jnp.float32
    ).astype(jnp.bfloat16)
    earlier = shifted_2(flux, "lat", 1)
    flux_window = jnp.concatenate([earlier, flux], axis=0)
    offsets = driving_air_latitude_index - (first_row - row_count)
    lower_rows = jnp.take(flux_window, offsets, axis=0)
    upper_rows = jnp.take(flux_window, offsets + 1, axis=0)
    forcing = 0.5 * (lower_rows.astype(jnp.float32) + upper_rows.astype(jnp.float32))
    wet_float = water_indicator.astype(jnp.float32)[:, None, :]
    push = jnp.einsum(
        "kf,rfl->rkl",
        driving_feature_matrix.astype(jnp.float32),
        forcing,
        precision=lax.Precision.HIGHEST,
    )
    forced = (marine_field.astype(jnp.float32) + wet_float * push).astype(jnp.bfloat16)
    padded = padded_2(forced, (("lat", 0),), 1)
    folded = jnp.take(forced[-1], seam_mirror_meridian, axis=1)
    top_row = jnp.where(band_index == band_count - 1, folded, padded[-1])
    extended = jnp.concatenate([padded[:-1], top_row[None]], axis=0)
    depth = depth_conv(extended, planar_stencil_coefficients, row_count)
    ocean_normed = channel_norm(depth, marine_rescale_factor).astype(jnp.bfloat16)
    hidden = tanh_gelu(
        jnp.einsum(
            "ek,rkl->rel", marine_expand_matrix, ocean_normed, preferred_element_type=jnp.float32
        )
    ).astype(jnp.bfloat16)
    update = jnp.einsum(
        "ke,rel->rkl", marine_contract_matrix, hidden, preferred_element_type=jnp.float32
    )
    marine_field_advanced = ((forced.astype(jnp.float32) + update) * wet_float).astype(jnp.bfloat16)
    skin_heat = marine_field_advanced[:, 0, :]
    following = shifted_2(skin_heat, "lat", -1)
    temp_window = jnp.concatenate([skin_heat, following], axis=0)
    skin_heat_aloft = jnp.take(temp_window, marine_latitude_beneath - first_row, axis=0)
    atm_normed = channel_norm(atmos_float, air_rescale_factor).astype(jnp.bfloat16)
    table = fourier_table(lon_count, MMAX)
    coefficients = jnp.einsum(
        "jcl,lm->jcm", atm_normed, table, preferred_element_type=jnp.float32
    ).astype(jnp.bfloat16)
    lat_table = latitude_table(row_count * band_count)
    gathered = lax.all_to_all(coefficients, "lat", split_axis=2, concat_axis=0, tiled=True)
    filtered_back = spectral_filtering(gathered, lat_table, spectral_order_damping)
    returned = lax.all_to_all(filtered_back, "lat", split_axis=0, concat_axis=2, tiled=True)
    grid_values = jnp.einsum("jcm,lm->jcl", returned, table, preferred_element_type=jnp.float32)
    activation = tanh_gelu(grid_values).astype(jnp.bfloat16)
    mixed = jnp.einsum(
        "dc,jcl->jdl", feature_blend_matrix, activation, preferred_element_type=jnp.float32
    )
    joint_outcome = (
        skin_heat_response[None, :, None] * skin_heat_aloft.astype(jnp.float32)[:, None, :]
    )
    atmosphere_next = (atmos_float + mixed + joint_outcome).astype(jnp.bfloat16)
    return (atmosphere_next, marine_field_advanced)


def solution(mesh):
    return jax.shard_map(
        local,
        mesh=mesh,
        in_specs=(
            P(("grp", "lat"), None, None),
            P(("grp", "lat"), None, None),
            P("lat", None),
            P(),
            P("lat"),
            P("lat"),
            P(),
            P(),
            P(),
            P(),
            P(),
            P(),
            P(),
            P(),
            P(),
            P(),
        ),
        out_specs=(P(("grp", "lat"), None, None), P(("grp", "lat"), None, None)),
        check_vma=False,
    )
```

profile of v0, /device:TPU:15, one launch (start us, length us, event | category | flops | bytes accessed | tf_op | source)
XLA Modules:
  0.0 178.8 jit_solution(11003746111985594327)
XLA Ops:
  0.7 3.1 %fusion.34 = bf16[3,8,1440]{2,1,0:T(8,128)(2,1)S(1)} fusion(bf16[3,384,1440]{1,2,0:T(8,128)(2,1)} %param.18, bf16[8,384]{1,0:T(8,128)(2,1)} %param.27), kind=kOutput, calls=%fused_computation.57 | convolution fusion | flops 26576640 | bytes 3393024 | tf_op jit(solution)/shard_map/fc,jcl->jfl/dot_general | solution.py:108
  3.7 3.8 %collective-permute-start = (bf16[3,8,1440]{2,1,0:T(8,128)(2,1)S(1)}, bf16[3,8,1440]{2,1,0:T(8,128)(2,1)S(1)}, u32[]{:S(2)}, u32[]{:S(2)}) collective-permute-start(bf16[3,8,1440]{2,1,0:T(8,128)(2,1)S(1)} %fusion.34), channel_id=1, source_target_pairs={{0,1},{1,2},{2,3},{3,4},{4,5},{5,6},{6,7},{7,8},{8,9},{9,10},{10,1... | collective-permute-start | bytes 207368 | tf_op jit(solution)/shard_map/ppermute | solution.py:18
  7.5 9.1 %fusion.40 = (f32[1440,384]{1,0:T(8,128)S(1)}, f32[1440,384]{1,0:T(8,128)S(1)}) fusion(), kind=kLoop, calls=%fused_computation.64 | loop fusion | flops 4976640 | bytes 4423680 | tf_op jit(solution)/shard_map/sin | solution.py:52
  17.4 2.0 %fusion.7 = f32[3,1440]{1,0:T(4,128)S(1)} fusion(bf16[3,384,1440]{1,2,0:T(8,128)(2,1)S(1)} %copy-done.1, f32[3,1440]{1,0:T(4,128)S(1)} %broadcast_multiply_fusion.1), kind=kLoop, calls=%fused_computation.17 | loop fusion | flops 6631200 | bytes 3352320 | tf_op jit(solution)/shard_map/reduce_sum | solution.py:43
  19.4 4.1 %fusion.52 = bf16[3,384,768]{2,1,0:T(8,128)(2,1)S(1)} fusion(bf16[3,384,1440]{1,2,0:T(8,128)(2,1)S(1)} %copy-done.1, f32[384]{0:T(512)S(1)} %copy-done.32, f32[3,1440]{1,0:T(4,128)S(1)} %add_rsqrt_fusion.1, f32[3,1440]{1,0:T(4,128)S(1)} %broadcast_multiply_fusion.1, f32[1440,384]{1,0:T(8,128)S(1)} %get-tuple-element.41, f32[1440,384]{1,0:T(8,128)S(1)} %get-tuple-element.42), kind=kOutput, calls=%fused_computation.76 | convolution fusion | flops 2560536576 | bytes 9547008 | tf_op jit(solution)/shard_map/jcl,lm->jcm/dot_general | solution.py:146
  23.5 3.3 %copy.28 = bf16[3,384,768]{1,0,2:T(4,128)(2,1)} copy(bf16[3,384,768]{2,1,0:T(8,128)(2,1)S(1)} %fusion.52) | data formatting | bytes 3538944 | tf_op jit(solution)/shard_map/convert_element_type | solution.py:148
  26.8 5.1 %all-to-all-start = ((bf16[3,384,768]{1,0,2:T(4,128)(2,1)}), bf16[3,384,768]{1,0,2:T(4,128)(2,1)}, u32[]{:S(2)}, u32[]{:S(2)}) async-start(bf16[3,384,768]{1,0,2:T(4,128)(2,1)} %copy.28), calls=%async_computation | async-start | bytes 4718592 | tf_op jit(solution)/shard_map/all_to_all | solution.py:150
  36.1 3.4 %fusion.28 = bf16[3,200,1440]{2,1,0:T(8,128)(2,1)S(1)} fusion(bf16[3,200,1440]{2,1,0:T(8,128)(2,1)} %param.19, f32[3,1440]{1,0:T(4,128)S(1)} %convert_element_type.98, bf16[3,8,1440]{2,1,0:T(8,128)(2,1)S(1)} %gather_fusion.3, bf16[3,8,1440]{2,1,0:T(8,128)(2,1)S(1)} %gather_fusion.2, pred[3]{0:T(512)(128)(4,1)S(1)} %get-tuple-element.37, ...), kind=kOutput, calls=%fused_computation.47 | convolution fusion | flops 86607360 | bytes 3614726 | tf_op jit(solution)/shard_map/kf,rfl->rkl/dot_general | solution.py:118
  39.4 1.3 fusion.128
  40.8 2.3 %collective-permute-start.2 = (bf16[1,200,1440]{2,1,0:T(8,128)(2,1)}, bf16[1,200,1440]{2,1,0:T(8,128)(2,1)}, u32[]{:S(2)}, u32[]{:S(2)}) collective-permute-start(bf16[1,200,1440]{2,1,0:T(8,128)(2,1)} %get-tuple-element.23), channel_id=1, source_target_pairs={{1,0},{2,1},{3,2},{4,3},{5,4},{6,5},{7,6},{8,7},{9,8},{10,9},{11,1... | collective-permute-start | bytes 1728008 | tf_op jit(solution)/shard_map/ppermute | solution.py:29
  43.1 4.1 %fusion.130 = (f32[3,200,1439]{2,1,0:T(8,128)}, f32[3,200,1439]{2,1,0:T(8,128)}) fusion(bf16[3,200,1440]{2,1,0:T(8,128)(2,1)S(1)} %fusion.28), kind=kLoop, calls=%fused_computation.157 | loop fusion | bytes 13814400 | tf_op jit(solution)/shard_map/jit(_roll_static)/slice | solution.py:68
  47.1 4.2 %collective-permute-start.1 = (bf16[1,200,1440]{2,1,0:T(8,128)(2,1)}, bf16[1,200,1440]{2,1,0:T(8,128)(2,1)S(1)}, u32[]{:S(2)}, u32[]{:S(2)}) collective-permute-start(bf16[1,200,1440]{2,1,0:T(8,128)(2,1)} %get-tuple-element.21), channel_id=1, source_target_pairs={{0,1},{1,2},{2,3},{3,4},{4,5},{5,6},{6,7},{7,8},{8,9},{9,10},{10,1... | collective-permute-start | bytes 1728008 | tf_op jit(solution)/shard_map/ppermute | solution.py:28
  52.2 1.3 copy.36
  53.5 5.7 %gather_fusion = bf16[1440,200]{1,0:T(8,128)(2,1)} fusion(bf16[200,1440]{0,1:T(8,128)(2,1)S(1)} %copy.36, s32[2048]{0:T(1024)} %pad_clamp_fusion), kind=kCustom, calls=%fused_computation.2 | custom fusion | bytes 1157760 | tf_op jit(solution)/shard_map/jit(_take)/gather | solution.py:126
  59.2 1.4 copy.37
  60.6 31.1 %collective-permute-done.2 = bf16[1,200,1440]{2,1,0:T(8,128)(2,1)} collective-permute-done((bf16[1,200,1440]{2,1,0:T(8,128)(2,1)}, bf16[1,200,1440]{2,1,0:T(8,128)(2,1)}, u32[]{:S(2)}, u32[]{:S(2)}) %collective-permute-start.2) | collective-permute-done | bytes 576032 | tf_op jit(solution)/shard_map/ppermute | solution.py:29
  91.7 1.2 fusion.57
  95.1 1.3 fusion.125
  96.6 4.8 %fusion.127 = (f32[3,200,1439]{2,1,0:T(8,128)}, f32[3,200,1439]{2,1,0:T(8,128)}) fusion(f32[3,200,1440]{2,1,0:T(8,128)S(1)} %get-tuple-element.20), kind=kLoop, calls=%fused_computation.154 | loop fusion | bytes 13814400 | tf_op jit(solution)/shard_map/jit(_roll_static)/slice | solution.py:68
  101.6 9.0 %fusion.122 = (f32[3,1440]{1,0:T(4,128)S(1)}, f32[3,200,1440]{2,1,0:T(8,128)}) fusion(f32[3,200,1]{2,1,0:T(8,128)} %get-tuple-element.16, f32[3,200,1439]{2,1,0:T(8,128)} %get-tuple-element.18, f32[200]{0:T(256)S(1)} %bitcast.89, bf16[1,200,1440]{2,1,0:T(8,128)(2,1)S(1)} %fusion.57, bf16[3,200,1440]{2,1,0:T(8,128)(2,1)S(1)} %fusion.28, f32[200]{0:T(256)S(1)} %bitcast.90, ...), kind=kLoop, calls=%fused_computation.150 | loop fusion | flops 25051680 | bytes 27096480 | tf_op jit(solution)/shard_map/reduce_sum | solution.py:41
  110.7 1.9 %copy.29 = bf16[3,384,768]{1,2,0:T(8,128)(2,1)S(1)} copy(bf16[3,384,768]{1,0,2:T(4,128)(2,1)} %all-to-all-done) | data formatting | bytes 3538944 | tf_op jit(solution)/shard_map/all_to_all | solution.py:150
  112.7 1.4 copy.30
  114.0 4.1 %convolution_convert_fusion.1 = bf16[48,384,48]{1,0,2:T(8,128)(2,1)} fusion(bf16[48,384,48]{1,2,0:T(8,128)(2,1)} %bitcast.77, f32[48,384]{1,0:T(8,128)S(1)} %copy-done.11, s32[48]{0:T(128)S(1)} %copy-done.27), kind=kOutput, calls=%fused_computation.75 | convolution fusion | flops 172574208 | bytes 3612864 | tf_op jit(solution)/shard_map/jl,lcm->jcm/dot_general | solution.py:79
  118.2 3.1 %copy.33 = bf16[48,384,48]{1,2,0:T(8,128)(2,1)} copy(bf16[48,384,48]{1,0,2:T(8,128)(2,1)} %convolution_convert_fusion.1) | data formatting | bytes 3538944 | tf_op jit(solution)/shard_map/convert_element_type | solution.py:81
  121.3 4.5 %all-to-all-start.1 = ((bf16[48,384,48]{1,2,0:T(8,128)(2,1)}), bf16[48,384,48]{1,2,0:T(8,128)(2,1)}, u32[]{:S(2)}, u32[]{:S(2)}) async-start(bf16[48,384,48]{1,2,0:T(8,128)(2,1)} %copy.33), calls=%async_computation.1 | async-start | bytes 3538944 | tf_op jit(solution)/shard_map/all_to_all | solution.py:152
  125.7 2.5 %multiply_reduce_fusion = f32[3,1440]{1,0:T(4,128)S(1)} fusion(f32[3,200,1440]{2,1,0:T(8,128)} %get-tuple-element.6, f32[3,1440]{1,0:T(4,128)S(1)} %broadcast_multiply_fusion), kind=kLoop, calls=%fused_computation.49 | loop fusion | flops 2587680 | bytes 3490560 | tf_op jit(solution)/shard_map/reduce_sum | solution.py:43
  128.3 9.0 %fusion.27 = bf16[3,200,1440]{2,1,0:T(8,128)(2,1)} fusion(f32[3,200,1440]{2,1,0:T(8,128)} %get-tuple-element.6, f32[3,1440]{1,0:T(4,128)S(1)} %copy-done.10, f32[200]{0:T(256)S(1)} %copy-done.34, f32[3,1440]{1,0:T(4,128)S(1)} %add_rsqrt_fusion, f32[3,1440]{1,0:T(4,128)S(1)} %broadcast_multiply_fusion, bf16[3,200,1440]{2,1,0:T(8,128)(2,1)S(1)} %fusion.28, ...), kind=kOutput, calls=%fused_computation.45 | convolution fusion | flops 2802816000 | bytes 7604640 | tf_op jit(solution)/shard_map/ke,rel->rkl/dot_general | solution.py:136
  137.3 1.0 slice.132
  138.4 2.2 %collective-permute-start.3 = (bf16[3,1440]{1,0:T(4,128)(2,1)S(1)}, bf16[3,1440]{1,0:T(4,128)(2,1)S(1)}, u32[]{:S(2)}, u32[]{:S(2)}) collective-permute-start(bf16[3,1440]{1,0:T(4,128)(2,1)S(1)} %bitcast.80), channel_id=1, source_target_pairs={{1,0},{2,1},{3,2},{4,3},{5,4},{6,5},{7,6},{8,7},{9,8},{10,9},{11,1... | collective-permute-start | bytes 25928 | tf_op jit(solution)/shard_map/ppermute | solution.py:18
  140.6 25.2 %collective-permute-done.3 = bf16[3,1440]{1,0:T(4,128)(2,1)S(1)} collective-permute-done((bf16[3,1440]{1,0:T(4,128)(2,1)S(1)}, bf16[3,1440]{1,0:T(4,128)(2,1)S(1)}, u32[]{:S(2)}, u32[]{:S(2)}) %collective-permute-start.3) | collective-permute-done | bytes 8672 | tf_op jit(solution)/shard_map/ppermute | solution.py:18
  166.5 2.9 %copy.34 = bf16[3,384,16,48]{1,3,2,0:T(8,128)(2,1)} copy(bf16[3,384,16,48]{1,3,0,2:T(8,128)(2,1)} %bitcast.7) | data formatting | bytes 3538944 | tf_op jit(solution)/shard_map/all_to_all | solution.py:152
  169.4 9.4 %fusion.11 = bf16[3,384,1440]{1,2,0:T(8,128)(2,1)} fusion(bf16[3,384,1440]{1,2,0:T(8,128)(2,1)} %param.18, f32[3,1440]{1,0:T(4,128)S(1)} %select_convert_fusion, f32[384]{0:T(512)S(1)} %copy-done.33, bf16[3,384,768]{1,2,0:T(8,128)(2,1)} %bitcast.79, f32[1440,384]{1,0:T(8,128)S(1)} %copy-done.5, f32[1440,384]{1,0:T(8,128)} %copy-done.6, ...), kind=kOutput, calls=%fused_computation.21 | convolution fusion | flops 3848601600 | bytes 13142400 | tf_op jit(solution)/shard_map/dc,jcl->jdl/dot_general | solution.py:155
  (100 shorter events, 8.9 us)
Async XLA Ops:
  0.6 127.7 %copy-start = (bf16[200,800]{1,0:T(8,128)(2,1)S(1)}, bf16[200,800]{1,0:T(8,128)(2,1)}, u32[]{:S(2)}) copy-start(bf16[200,800]{1,0:T(8,128)(2,1)} %param.33) | copy-start | bytes 960004
  0.6 16.0 %copy-start.1 = (bf16[3,384,1440]{1,2,0:T(8,128)(2,1)S(1)}, bf16[3,384,1440]{1,2,0:T(8,128)(2,1)}, u32[]{:S(2)}) copy-start(bf16[3,384,1440]{1,2,0:T(8,128)(2,1)} %param.18) | copy-start | bytes 9953284
  3.7 31.2 %collective-permute-start = (bf16[3,8,1440]{2,1,0:T(8,128)(2,1)S(1)}, bf16[3,8,1440]{2,1,0:T(8,128)(2,1)S(1)}, u32[]{:S(2)}, u32[]{:S(2)}) collective-permute-start(bf16[3,8,1440]{2,1,0:T(8,128)(2,1)S(1)} %fusion.34), channel_id=1, source_target_pairs={{0,1},{1,2},{2,3},{3,4},{4,5},{5,6},{6,7},{7,8},{8,9},{9,10},{10,1... | collective-permute-start | bytes 207368 | tf_op jit(solution)/shard_map/ppermute | solution.py:18
  23.4 8.5 %copy-start.12 = (s32[1440]{0:T(1024)S(1)}, s32[1440]{0:T(1024)}, u32[]{:S(2)}) copy-start(s32[1440]{0:T(1024)} %param.21) | copy-start | bytes 17284
  23.5 9.1 %copy-start.13 = (s32[3,1440]{1,0:T(4,128)S(1)}, s32[3,1440]{1,0:T(4,128)}, u32[]{:S(2)}) copy-start(s32[3,1440]{1,0:T(4,128)} %param.20) | copy-start | bytes 51844
  23.5 9.7 %copy-start.14 = (f32[9,200]{1,0:T(8,128)S(1)}, f32[9,200]{1,0:T(8,128)}, u32[]{:S(2)}) copy-start(f32[9,200]{1,0:T(8,128)} %param.30) | copy-start | bytes 21604
  23.5 10.3 %copy-start.28 = (s32[3]{0:T(128)S(1)}, s32[3]{0:T(128)}, u32[]{:S(2)}) copy-start(s32[3]{0:T(128)} %param.23) | copy-start | bytes 40
  23.5 10.9 %copy-start.29 = (s32[3]{0:T(128)S(1)}, s32[3]{0:T(128)}, u32[]{:S(2)}) copy-start(s32[3]{0:T(128)} %param.22) | copy-start | bytes 40
  26.8 9.3 %copy-start.15 = (bf16[200,8]{0,1:T(8,128)(2,1)S(1)}, bf16[200,8]{0,1:T(8,128)(2,1)}, u32[]{:S(2)}) copy-start(bf16[200,8]{0,1:T(8,128)(2,1)} %param.29) | copy-start | bytes 9604
  26.8 83.9 %all-to-all-start = ((bf16[3,384,768]{1,0,2:T(4,128)(2,1)}), bf16[3,384,768]{1,0,2:T(4,128)(2,1)}, u32[]{:S(2)}, u32[]{:S(2)}) async-start(bf16[3,384,768]{1,0,2:T(4,128)(2,1)} %copy.28), calls=%async_computation | async-start | bytes 4718592 | tf_op jit(solution)/shard_map/all_to_all | solution.py:150
  32.5 8.2 %copy-start.9 = (f32[3,1440]{1,0:T(4,128)}, f32[3,1440]{1,0:T(4,128)S(1)}, u32[]{:S(2)}) copy-start(f32[3,1440]{1,0:T(4,128)S(1)} %convert_element_type.98) | copy-start | bytes 51844
  40.8 50.9 %collective-permute-start.2 = (bf16[1,200,1440]{2,1,0:T(8,128)(2,1)}, bf16[1,200,1440]{2,1,0:T(8,128)(2,1)}, u32[]{:S(2)}, u32[]{:S(2)}) collective-permute-start(bf16[1,200,1440]{2,1,0:T(8,128)(2,1)} %get-tuple-element.23), channel_id=1, source_target_pairs={{1,0},{2,1},{3,2},{4,3},{5,4},{6,5},{7,6},{8,7},{9,8},{10,9},{11,1... | collective-permute-start | bytes 1728008 | tf_op jit(solution)/shard_map/ppermute | solution.py:29
  47.1 45.7 %collective-permute-start.1 = (bf16[1,200,1440]{2,1,0:T(8,128)(2,1)}, bf16[1,200,1440]{2,1,0:T(8,128)(2,1)S(1)}, u32[]{:S(2)}, u32[]{:S(2)}) collective-permute-start(bf16[1,200,1440]{2,1,0:T(8,128)(2,1)} %get-tuple-element.21), channel_id=1, source_target_pairs={{0,1},{1,2},{2,3},{3,4},{4,5},{5,6},{6,7},{7,8},{8,9},{9,10},{10,1... | collective-permute-start | bytes 1728008 | tf_op jit(solution)/shard_map/ppermute | solution.py:28
  96.5 5.1 %copy-start.8 = (f32[3,200,1]{2,1,0:T(8,128)S(1)}, f32[3,200,1]{2,1,0:T(8,128)}, u32[]{:S(2)}) copy-start(f32[3,200,1]{2,1,0:T(8,128)} %get-tuple-element.25) | copy-start | bytes 7204
  96.5 5.1 %copy-start.16 = (f32[1,200]{1,0:T(1,128)S(1)}, f32[1,200]{1,0:T(1,128)}, u32[]{:S(2)}) copy-start(f32[1,200]{1,0:T(1,128)} %get-tuple-element.28) | copy-start | bytes 2404
  96.5 5.1 %copy-start.17 = (f32[1,200]{1,0:T(1,128)S(1)}, f32[1,200]{1,0:T(1,128)}, u32[]{:S(2)}) copy-start(f32[1,200]{1,0:T(1,128)} %get-tuple-element.29) | copy-start | bytes 2404
  96.5 5.1 %copy-start.18 = (f32[1,200]{1,0:T(1,128)S(1)}, f32[1,200]{1,0:T(1,128)}, u32[]{:S(2)}) copy-start(f32[1,200]{1,0:T(1,128)} %get-tuple-element.30) | copy-start | bytes 2404
  96.5 5.1 %copy-start.19 = (f32[1,200]{1,0:T(1,128)S(1)}, f32[1,200]{1,0:T(1,128)}, u32[]{:S(2)}) copy-start(f32[1,200]{1,0:T(1,128)} %get-tuple-element.31) | copy-start | bytes 2404
  96.5 5.1 %copy-start.20 = (f32[1,200]{1,0:T(1,128)S(1)}, f32[1,200]{1,0:T(1,128)}, u32[]{:S(2)}) copy-start(f32[1,200]{1,0:T(1,128)} %get-tuple-element.32) | copy-start | bytes 2404
  96.5 5.1 %copy-start.21 = (f32[1,200]{1,0:T(1,128)S(1)}, f32[1,200]{1,0:T(1,128)}, u32[]{:S(2)}) copy-start(f32[1,200]{1,0:T(1,128)} %get-tuple-element.33) | copy-start | bytes 2404
  96.5 5.1 %copy-start.22 = (f32[1,200]{1,0:T(1,128)S(1)}, f32[1,200]{1,0:T(1,128)}, u32[]{:S(2)}) copy-start(f32[1,200]{1,0:T(1,128)} %get-tuple-element.34) | copy-start | bytes 2404
  96.5 5.1 %copy-start.23 = (f32[1,200]{1,0:T(1,128)S(1)}, f32[1,200]{1,0:T(1,128)}, u32[]{:S(2)}) copy-start(f32[1,200]{1,0:T(1,128)} %get-tuple-element.35) | copy-start | bytes 2404
  121.3 7.0 %copy-start.10 = (f32[3,1440]{1,0:T(4,128)S(1)}, f32[3,1440]{1,0:T(4,128)}, u32[]{:S(2)}) copy-start(f32[3,1440]{1,0:T(4,128)} %copy-done.9) | copy-start | bytes 51844
  121.3 7.0 %copy-start.30 = (bf16[800,200]{0,1:T(8,128)(2,1)S(1)}, bf16[800,200]{0,1:T(8,128)(2,1)}, u32[]{:S(2)}) copy-start(bf16[800,200]{0,1:T(8,128)(2,1)} %param.32) | copy-start | bytes 960004
  121.3 7.0 %copy-start.34 = (f32[200]{0:T(256)S(1)}, f32[200]{0:T(256)}, u32[]{:S(2)}) copy-start(f32[200]{0:T(256)} %param.31) | copy-start | bytes 2404
  121.3 45.2 %all-to-all-start.1 = ((bf16[48,384,48]{1,2,0:T(8,128)(2,1)}), bf16[48,384,48]{1,2,0:T(8,128)(2,1)}, u32[]{:S(2)}, u32[]{:S(2)}) async-start(bf16[48,384,48]{1,2,0:T(8,128)(2,1)} %copy.33), calls=%async_computation.1 | async-start | bytes 3538944 | tf_op jit(solution)/shard_map/all_to_all | solution.py:152
  128.3 12.3 %copy-start.26 = (s32[3]{0:T(128)S(1)}, s32[3]{0:T(128)}, u32[]{:S(2)}) copy-start(s32[3]{0:T(128)} %get-tuple-element.4) | copy-start | bytes 40
  128.3 38.1 %copy-start.25 = (pred[3]{0:T(512)(128)(4,1)S(1)}, pred[3]{0:T(512)(128)(4,1)}, u32[]{:S(2)}) copy-start(pred[3]{0:T(512)(128)(4,1)} %get-tuple-element.3) | copy-start | bytes 13
  137.3 32.0 %copy-start.5 = (f32[1440,384]{1,0:T(8,128)S(1)}, f32[1440,384]{1,0:T(8,128)}, u32[]{:S(2)}) copy-start(f32[1440,384]{1,0:T(8,128)} %copy-done.4) | copy-start | bytes 6635524
  137.3 32.1 %copy-start.31 = (bf16[384,384]{1,0:T(8,128)(2,1)S(1)}, bf16[384,384]{1,0:T(8,128)(2,1)}, u32[]{:S(2)}) copy-start(bf16[384,384]{1,0:T(8,128)(2,1)} %param.26) | copy-start | bytes 884740
  137.3 32.1 %copy-start.33 = (f32[384]{0:T(512)S(1)}, f32[384]{0:T(512)}, u32[]{:S(2)}) copy-start(f32[384]{0:T(512)} %param.28) | copy-start | bytes 4612
  138.4 27.4 %collective-permute-start.3 = (bf16[3,1440]{1,0:T(4,128)(2,1)S(1)}, bf16[3,1440]{1,0:T(4,128)(2,1)S(1)}, u32[]{:S(2)}, u32[]{:S(2)}) collective-permute-start(bf16[3,1440]{1,0:T(4,128)(2,1)S(1)} %bitcast.80), channel_id=1, source_target_pairs={{1,0},{2,1},{3,2},{4,3},{5,4},{6,5},{7,6},{8,7},{9,8},{10,9},{11,1... | collective-permute-start | bytes 25928 | tf_op jit(solution)/shard_map/ppermute | solution.py:18
  (9 other events, 34.9 us)
where the time goes:
time: 180 us; the launch traced here: 179 us
  waiting for transfers between devices  56.3 us (31%)
  local copies, waits for them, and re-layouts  38.8 us (22%)
  matrix products  33 us (18%)
  other arithmetic  27.5 us (15%)
  starting transfers between devices  21.9 us (12%)
    ppermute x1, waiting for transfers between devices, padded_2(): after = lax.ppermute(leading, axis, down)  31.1 us
    ppermute x2, waiting for transfers between devices, shifted_2(): return lax.ppermute(array, axis, pairs)  25.2 us
    slice x6, local copies, waits for them, and re-layouts, depth_conv(): shifted = jnp.roll(row_band, 1 - horizontal, axis=2)  12.8 us
    reduce_sum x2, other arithmetic, channel_norm(): average = jnp.mean(values, axis=-2, keepdims=True)  9.74 us
    dot_general x1, matrix products, local(): jnp.einsum('dc,jcl->jdl', feature_blend_matrix, activation, preferred_ele...  9.4 us
    sin x1, other arithmetic, fourier_table(): jnp.sin(angles)  9.11 us
    dot_general x1, matrix products, local(): jnp.einsum('ke,rel->rkl', marine_contract_matrix, hidden, preferred_eleme...  8.99 us
    gather x2, local copies, waits for them, and re-layouts, local(): folded = jnp.take(forced[-1], seam_mirror_meridian, axis=1)  7.08 us
  transfers between devices with their start and end apart: 6, of which 2 were waited for; matrix products, arithmetic and copies ran while one was open for 41% of the time, Pallas kernels for 0%

commit v1 on v0

v1 whole, which is shorter than its diff:
```python
import math

import jax
import jax.numpy as jnp
import numpy as np
from jax import lax
from jax.experimental import pallas as pl
from jax.experimental.pallas import tpu as pltpu
from jax.sharding import PartitionSpec as P

MMAX = 384


EPSILON = 1e-05
GELU_SCALE = 0.7978845608028654
GROUP = 16


def shifted_2(array, axis, by):
    size = lax.axis_size(axis)
    pairs = [(i, i + by) for i in range(size) if 0 <= i + by < size]
    return lax.ppermute(array, axis, pairs)


def halo_rows(array, axis):
    size = lax.axis_size(axis)
    up = [(i, i + 1) for i in range(size - 1)]
    down = [(j, i) for i, j in up]
    before = lax.ppermute(array[-1:], axis, up)
    after = lax.ppermute(array[:1], axis, down)
    return before, after


def tanh_gelu(values):
    return (
        0.5 * values * (1.0 + jnp.tanh(GELU_SCALE * (values + 0.044715 * values * values * values)))
    )


def channel_norm(values, gain):
    average = jnp.mean(values, axis=-2, keepdims=True)
    centered = values - average
    variance = jnp.mean(centered * centered, axis=-2, keepdims=True)
    return centered * lax.rsqrt(variance + EPSILON) * gain[:, None]


def fourier_rows(lon_count, mode_count):
    phase = np.arange(mode_count)[:, None] * np.arange(lon_count)[None, :] % lon_count
    angles = 2.0 * math.pi / lon_count * phase
    table = np.concatenate([np.cos(angles), np.sin(angles)], axis=0) / math.sqrt(lon_count)
    return table.astype(jnp.bfloat16)


def latitude_values(row_count):
    index = np.arange(row_count)
    phase = (2 * index[:, None] + 1) * index[None, :] % (4 * row_count)
    angles = math.pi / (2.0 * row_count) * phase
    return (np.cos(angles) * math.sqrt(2.0 / row_count)).astype(jnp.bfloat16)


def latitude_blocks(bands, rows):
    values = latitude_values(bands * rows).astype(np.float32).reshape(bands, rows, bands * rows)
    same = np.eye(GROUP, dtype=np.float32)
    full = np.einsum("bjl,pq->lpjbq", values, same)
    return full.reshape(bands * rows * GROUP, rows * bands * GROUP).astype(jnp.bfloat16)


def forward_kernel(x_ref, table_ref, gain_ref, exchange_ref, coef_ref, flux_ref):
    raw = x_ref[0]
    flux_ref[0] = lax.dot_general(
        exchange_ref[...], raw, (((1,), (1,)), ((), ())), preferred_element_type=jnp.float32
    ).astype(jnp.bfloat16)
    values = raw.astype(jnp.float32)
    average = jnp.mean(values, axis=-1, keepdims=True)
    centered = values - average
    variance = jnp.mean(centered * centered, axis=-1, keepdims=True)
    normed = (centered * lax.rsqrt(variance + EPSILON) * gain_ref[...]).astype(jnp.bfloat16)
    coef_ref[...] = jnp.dot(
        table_ref[...], normed, preferred_element_type=jnp.float32
    ).astype(jnp.bfloat16)


def forward_transform(air_rows, table, gain, exchange):
    rows, lon_count, channels = air_rows.shape
    modes, fields = table.shape[0], exchange.shape[0]
    return pl.pallas_call(
        forward_kernel,
        grid=(rows,),
        in_specs=[
            pl.BlockSpec((1, lon_count, channels), lambda j: (j, 0, 0)),
            pl.BlockSpec((modes, lon_count), lambda j: (0, 0)),
            pl.BlockSpec((1, channels), lambda j: (0, 0)),
            pl.BlockSpec((fields, channels), lambda j: (0, 0)),
        ],
        out_specs=[
            pl.BlockSpec((modes, channels), lambda j: (0, j)),
            pl.BlockSpec((1, fields, lon_count), lambda j: (j, 0, 0)),
        ],
        out_shape=[
            jax.ShapeDtypeStruct((modes, rows * channels), jnp.bfloat16),
            jax.ShapeDtypeStruct((rows, fields, lon_count), jnp.bfloat16),
        ],
        cost_estimate=pl.CostEstimate(
            flops=2 * rows * lon_count * channels * modes,
            bytes_accessed=2 * (rows * lon_count * channels + modes * (lon_count + rows * channels)),
            transcendentals=0,
        ),
    )(air_rows, table, gain[None, :], exchange)


def filter_kernel(got_ref, blocks_ref, back_ref, damping_ref, out_ref):
    bands, group, lanes = got_ref.shape
    depth = bands * group
    rows = blocks_ref.shape[1] // depth
    channels = lanes // rows
    spectrum = jnp.zeros((blocks_ref.shape[0], channels), jnp.float32)
    for j in range(rows):
        part = got_ref[:, :, j * channels : (j + 1) * channels].reshape(depth, channels)
        spectrum = spectrum + jnp.dot(
            blocks_ref[:, j * depth : (j + 1) * depth], part, preferred_element_type=jnp.float32
        )
    filtered = (spectrum * damping_ref[...]).astype(jnp.bfloat16)
    for j in range(rows):
        back = jnp.dot(
            back_ref[j * depth : (j + 1) * depth, :], filtered, preferred_element_type=jnp.float32
        )
        out_ref[:, :, j * channels : (j + 1) * channels] = back.astype(jnp.bfloat16).reshape(
            bands, group, channels
        )


def latitude_filter(gathered, damping, rows):
    bands, own, lanes = gathered.shape
    channels = lanes // rows
    if own % GROUP or bands > GROUP:
        split = gathered.reshape(bands, own, rows, channels)
        table = jnp.asarray(latitude_values(bands * rows)).reshape(bands, rows, bands * rows)
        spectrum = jnp.einsum("bjl,bqjc->lqc", table, split, preferred_element_type=jnp.float32)
        filtered = (spectrum * damping[:, None, :]).astype(jnp.bfloat16)
        back = jnp.einsum("bjl,lqc->bqjc", table, filtered, preferred_element_type=jnp.float32)
        return back.astype(jnp.bfloat16).reshape(gathered.shape)
    blocks = lax.optimization_barrier(jnp.asarray(latitude_blocks(bands, rows)))
    side = blocks.shape[0]
    damping_rows = jnp.repeat(damping, GROUP, axis=0)
    return pl.pallas_call(
        filter_kernel,
        grid=(own // GROUP,),
        in_specs=[
            pl.BlockSpec((bands, GROUP, lanes), lambda g: (0, g, 0)),
            pl.BlockSpec((side, side), lambda g: (0, 0)),
            pl.BlockSpec((side, side), lambda g: (0, 0)),
            pl.BlockSpec((side, channels), lambda g: (0, 0)),
        ],
        out_specs=pl.BlockSpec((bands, GROUP, lanes), lambda g: (0, g, 0)),
        out_shape=jax.ShapeDtypeStruct(gathered.shape, jnp.bfloat16),
        cost_estimate=pl.CostEstimate(
            flops=4 * side * side * channels * (own // GROUP),
            bytes_accessed=4 * gathered.size + 4 * side * side,
            transcendentals=0,
        ),
    )(gathered, blocks, blocks.T, damping_rows)


def inverse_kernel(back_ref, table_ref, blend_ref, x_ref, sst_ref, skin_ref, out_ref):
    grid_values = jnp.dot(table_ref[...], back_ref[...], preferred_element_type=jnp.float32)
    activation = tanh_gelu(grid_values).astype(jnp.bfloat16)
    mixed = lax.dot_general(
        activation, blend_ref[...], (((1,), (1,)), ((), ())), preferred_element_type=jnp.float32
    )
    skin = skin_ref[...]
    high = skin.astype(jnp.bfloat16).astype(jnp.float32)
    middle = (skin - high).astype(jnp.bfloat16).astype(jnp.float32)
    low = skin - high - middle
    level = lax.broadcasted_iota(jnp.int32, (8, skin.shape[1]), 0)
    pieces = jnp.where(
        level == 0, high, jnp.where(level == 1, middle, jnp.where(level == 2, low, 0.0))
    ).astype(jnp.bfloat16)
    warmth = jnp.broadcast_to(sst_ref[0].astype(jnp.float32), (8, sst_ref.shape[2]))
    joint = lax.dot_general(
        warmth.astype(jnp.bfloat16),
        pieces,
        (((0,), (0,)), ((), ())),
        preferred_element_type=jnp.float32,
    )
    out_ref[0] = (x_ref[0].astype(jnp.float32) + mixed + joint).astype(jnp.bfloat16)


def inverse_transform(returned, table, blend, air_rows, sst, skin):
    rows, lon_count, channels = air_rows.shape
    modes = table.shape[1]
    return pl.pallas_call(
        inverse_kernel,
        grid=(rows,),
        in_specs=[
            pl.BlockSpec((modes, channels), lambda j: (0, j)),
            pl.BlockSpec((lon_count, modes), lambda j: (0, 0)),
            pl.BlockSpec((channels, channels), lambda j: (0, 0)),
            pl.BlockSpec((1, lon_count, channels), lambda j: (j, 0, 0)),
            pl.BlockSpec((1, 1, lon_count), lambda j: (j, 0, 0)),
            pl.BlockSpec((1, channels), lambda j: (0, 0)),
        ],
        out_specs=pl.BlockSpec((1, lon_count, channels), lambda j: (j, 0, 0)),
        out_shape=jax.ShapeDtypeStruct(air_rows.shape, jnp.bfloat16),
        cost_estimate=pl.CostEstimate(
            flops=2 * rows * lon_count * channels * (modes + channels),
            bytes_accessed=4 * rows * lon_count * channels + 2 * modes * (lon_count + channels),
            transcendentals=rows * lon_count * channels,
        ),
    )(returned, table, blend, air_rows, sst[:, None, :], skin[None, :])


def depth_conv(extended, planar_stencil_coefficients, row_count):
    summed = jnp.zeros((row_count,) + extended.shape[1:], jnp.float32)
    for vertical in range(3):
        row_band = extended[vertical : vertical + row_count].astype(jnp.float32)
        for horizontal in range(3):
            shifted = jnp.roll(row_band, 1 - horizontal, axis=2)
            summed = (
                summed
                + planar_stencil_coefficients[3 * vertical + horizontal][None, :, None] * shifted
            )
    return summed


def local(
    air_field,
    marine_field,
    water_indicator,
    seam_mirror_meridian,
    driving_air_latitude_index,
    marine_latitude_beneath,
    air_rescale_factor,
    spectral_order_damping,
    feature_blend_matrix,
    boundary_exchange_matrix,
    skin_heat_response,
    driving_feature_matrix,
    planar_stencil_coefficients,
    marine_rescale_factor,
    marine_expand_matrix,
    marine_contract_matrix,
):
    row_count, channels, lon_count = air_field.shape
    band_count = lax.axis_size("lat")
    band_index = lax.axis_index("lat")
    first_row = band_index * row_count
    air_rows = air_field.transpose(0, 2, 1)
    table = lax.optimization_barrier(jnp.asarray(fourier_rows(lon_count, MMAX)))
    modes = table.shape[0]
    coefficients, flux = forward_transform(
        air_rows, table, air_rescale_factor, boundary_exchange_matrix
    )
    gathered = lax.all_to_all(coefficients, "lat", split_axis=0, concat_axis=0, tiled=True)

    earlier = shifted_2(flux, "lat", 1)
    flux_window = jnp.concatenate([earlier, flux], axis=0)
    offsets = driving_air_latitude_index - (first_row - row_count)
    lower_rows = jnp.take(flux_window, offsets, axis=0)
    upper_rows = jnp.take(flux_window, offsets + 1, axis=0)
    forcing = 0.5 * (lower_rows.astype(jnp.float32) + upper_rows.astype(jnp.float32))
    wet_float = water_indicator.astype(jnp.float32)[:, None, :]
    push = jnp.einsum(
        "kf,rfl->rkl",
        driving_feature_matrix.astype(jnp.float32),
        forcing,
        precision=lax.Precision.HIGHEST,
    )
    forced = (marine_field.astype(jnp.float32) + wet_float * push).astype(jnp.bfloat16)
    before, after = halo_rows(forced, "lat")
    folded = jnp.take(forced[-1], seam_mirror_meridian, axis=1)

    filtered_back = latitude_filter(
        gathered.reshape(band_count, modes // band_count, row_count * channels),
        spectral_order_damping,
        row_count,
    )
    returned = lax.all_to_all(
        filtered_back.reshape(modes, row_count * channels),
        "lat",
        split_axis=0,
        concat_axis=0,
        tiled=True,
    )

    before, after, folded, _ = lax.optimization_barrier(
        (before, after, folded, filtered_back[0, 0, 0])
    )
    top_row = jnp.where(band_index == band_count - 1, folded[None], after)
    extended = jnp.concatenate([before, forced, top_row], axis=0)
    depth = depth_conv(extended, planar_stencil_coefficients, row_count)
    ocean_normed = channel_norm(depth, marine_rescale_factor).astype(jnp.bfloat16)
    hidden = tanh_gelu(
        jnp.einsum(
            "ek,rkl->rel", marine_expand_matrix, ocean_normed, preferred_element_type=jnp.float32
        )
    ).astype(jnp.bfloat16)
    update = jnp.einsum(
        "ke,rel->rkl", marine_contract_matrix, hidden, preferred_element_type=jnp.float32
    )
    marine_field_advanced = ((forced.astype(jnp.float32) + update) * wet_float).astype(jnp.bfloat16)
    skin_heat = marine_field_advanced[:, 0, :]
    following = shifted_2(skin_heat, "lat", -1)
    temp_window = jnp.concatenate([skin_heat, following], axis=0)
    skin_heat_aloft = jnp.take(temp_window, marine_latitude_beneath - first_row, axis=0)

    outcome = inverse_transform(
        returned, table.T, feature_blend_matrix, air_rows, skin_heat_aloft, skin_heat_response
    )
    return (outcome.transpose(0, 2, 1), marine_field_advanced)


def solution(mesh):
    return jax.shard_map(
        local,
        mesh=mesh,
        in_specs=(
            P(("grp", "lat"), None, None),
            P(("grp", "lat"), None, None),
            P("lat", None),
            P(),
            P("lat"),
            P("lat"),
            P(),
            P(),
            P(),
            P(),
            P(),
            P(),
            P(),
            P(),
            P(),
            P(),
        ),
        out_specs=(P(("grp", "lat"), None, None), P(("grp", "lat"), None, None)),
        check_vma=False,
    )
```

time: 180 us -> 155 us (0.86)
  Pallas kernels: 0 us -> 25.9 us
  matrix products: 33 us -> 12.4 us
  waiting for transfers between devices: 56.3 us -> 41.7 us
  other arithmetic: 27.5 us -> 16.9 us
  local copies, waits for them, and re-layouts: 38.8 us -> 34.7 us
    pallas_call x0 -> x3, Pallas kernels: none -> 25.9 us  [the longest x1 10.5 us: inverse_transform(): pl.pallas_call(inverse_kernel, grid=(rows,), in_specs=[pl.BlockSpec((mode...]
    dot_general x4 -> x0, matrix products: 20.7 us -> none  [the longest x1 9.4 us: local(): jnp.einsum('dc,jcl->jdl', feature_blend_matrix, activation, preferred_ele...]
    ppermute x2, waiting for transfers between devices: 31.1 us -> 16.7 us  [the longest x1 15 us: halo_rows(): before = lax.ppermute(array[-1:], axis, up)]
    sin x1 -> x0, other arithmetic: 9.11 us -> none  [fourier_table(): jnp.sin(angles)]
    convert_element_type x2 -> x0, local copies, waits for them, and re-layouts: 6.37 us -> none  [the longest x1 3.3 us: local(): coefficients = jnp.einsum('jcl,lm->jcm', atm_normed, table, preferred_ele...]
    all_to_all x3 -> x0, local copies, waits for them, and re-layouts: 6.19 us -> none  [the longest x2 3.32 us: local(): lax.all_to_all(coefficients, 'lat', split_axis=2, concat_axis=0, tiled=True)]
    optimization_barrier x0 -> x2, local copies, waits for them, and re-layouts: none -> 5.75 us  [the longest x1 4.29 us: local(): table = lax.optimization_barrier(jnp.asarray(fourier_rows(lon_count, MMAX)))]
    broadcast_in_dim x0 -> x3, local copies, waits for them, and re-layouts: none -> 2.23 us  [the longest x1 1.09 us: latitude_filter(): damping_rows = jnp.repeat(damping, GROUP, axis=0)]
  transfers between devices with their start and end apart: 6 -> 6, of which waited for: 2 -> 3; matrix products, arithmetic and copies ran while one was open for 41% -> 38% of each run, Pallas kernels for 0% -> 0%
where the time goes in v1:
time: 155 us; the launch traced here: 154 us
  waiting for transfers between devices  41.7 us (27%)
  local copies, waits for them, and re-layouts  34.7 us (22%)
  Pallas kernels  25.9 us (17%)
  starting transfers between devices  21.1 us (14%)
  other arithmetic  16.9 us (11%)
  matrix products  12.4 us (8%)
    ppermute x2, waiting for transfers between devices, shifted_2(): return lax.ppermute(array, axis, pairs)  25 us
    ppermute x1, waiting for transfers between devices, halo_rows(): before = lax.ppermute(array[-1:], axis, up)  15 us
    slice x6, local copies, waits for them, and re-layouts, depth_conv(): shifted = jnp.roll(row_band, 1 - horizontal, axis=2)  12.9 us
    pallas_call x1, Pallas kernels, inverse_transform(): pl.pallas_call(inverse_kernel, grid=(rows,), in_specs=[pl.BlockSpec((mode...  10.5 us
    dot_general x1, matrix products, local(): jnp.einsum('ke,rel->rkl', marine_contract_matrix, hidden, preferred_eleme...  8.99 us
    reduce_sum x1, other arithmetic, channel_norm(): average = jnp.mean(values, axis=-2, keepdims=True)  8.96 us
    pallas_call x1, Pallas kernels, forward_transform(): pl.pallas_call(forward_kernel, grid=(rows,), in_specs=[pl.BlockSpec((1, l...  8.16 us
    gather x2, local copies, waits for them, and re-layouts, local(): folded = jnp.take(forced[-1], seam_mirror_meridian, axis=1)  7.7 us
  transfers between devices with their start and end apart: 6, of which 3 were waited for; matrix products, arithmetic and copies ran while one was open for 38% of the time, Pallas kernels for 0%

profile of v1, /device:TPU:15, one launch (start us, length us, event | category | flops | bytes accessed | tf_op | source)
XLA Modules:
  0.0 153.7 jit_solution(10237830394053280348)
XLA Ops:
  0.7 4.3 %copy.24.table_ref = bf16[768,1440]{1,0:T(8,128)(2,1)} copy(bf16[768,1440]{0,1:T(8,128)(2,1)} %constant.73.clone) | data formatting | bytes 4423680 | tf_op jit(solution)/shard_map/optimization_barrier | solution.py:248
  5.5 8.2 %shard_map.185 = (bf16[768,1152]{1,0:T(8,128)(2,1)}, bf16[3,8,1440]{2,1,0:T(8,128)(2,1)}) custom-call(bf16[3,1440,384]{2,1,0:T(8,128)(2,1)} %bitcast.69, bf16[768,1440]{1,0:T(8,128)(2,1)} %copy.24.table_ref, f32[1,384]{1,0:T(1,128)} %broadcast_in_dim.49.gain_ref, bf16[8,384]{1,0:T(8,128)(2,1)} %exchange_ref.1), custom_call_target="tpu_custom_call" | custom-call | flops 2548039680 | bytes 7299072 | tf_op jit(solution)/shard_map/pallas_call | solution.py:86
  13.7 3.9 %collective-permute-start = (bf16[3,8,1440]{2,1,0:T(8,128)(2,1)}, bf16[3,8,1440]{2,1,0:T(8,128)(2,1)S(1)}, u32[]{:S(2)}, u32[]{:S(2)}) collective-permute-start(bf16[3,8,1440]{2,1,0:T(8,128)(2,1)} %get-tuple-element.9), channel_id=1, source_target_pairs={{0,1},{1,2},{2,3},{3,4},{4,5},{5,6},{6,7},{7,8},{8,9},{9,10},{10,1... | collective-permute-start | bytes 207368 | tf_op jit(solution)/shard_map/ppermute | solution.py:22
  17.6 5.0 %all-to-all-start = ((bf16[16,48,1152]{2,1,0:T(8,128)(2,1)}), bf16[16,48,1152]{2,1,0:T(8,128)(2,1)}, u32[]{:S(2)}, u32[]{:S(2)}) async-start(bf16[16,48,1152]{2,1,0:T(8,128)(2,1)} %bitcast.54), calls=%async_computation | async-start | bytes 3538944 | tf_op jit(solution)/shard_map/all_to_all | solution.py:253
  25.0 1.5 copy.25.blocks_ref
  27.7 3.4 %fusion.15 = bf16[3,200,1440]{2,1,0:T(8,128)(2,1)S(1)} fusion(bf16[3,200,1440]{2,1,0:T(8,128)(2,1)} %param.21, f32[3,1440]{1,0:T(4,128)S(1)} %convert_element_type.36, bf16[3,8,1440]{2,1,0:T(8,128)(2,1)S(1)} %gather_fusion.3, bf16[3,8,1440]{2,1,0:T(8,128)(2,1)S(1)} %gather_fusion.2, pred[3]{0:T(512)(128)(4,1)S(1)} %get-tuple-element.47, ...), kind=kOutput, calls=%fused_computation.29 | convolution fusion | flops 86607360 | bytes 3614726 | tf_op jit(solution)/shard_map/kf,rfl->rkl/dot_general | solution.py:262
  31.1 1.3 slice_bitcast_fusion
  32.4 4.0 %fusion.51 = (f32[3,200,1439]{2,1,0:T(8,128)}, f32[3,200,1439]{2,1,0:T(8,128)}) fusion(bf16[3,200,1440]{2,1,0:T(8,128)(2,1)S(1)} %fusion.15), kind=kLoop, calls=%fused_computation.86 | loop fusion | bytes 13814400 | tf_op jit(solution)/shard_map/jit(_roll_static)/slice | solution.py:217
  36.4 3.4 %collective-permute-start.1 = (bf16[1,200,1440]{2,1,0:T(8,128)(2,1)}, bf16[1,200,1440]{2,1,0:T(8,128)(2,1)S(1)}, u32[]{:S(2)}, u32[]{:S(2)}) collective-permute-start(bf16[1,200,1440]{2,1,0:T(8,128)(2,1)} %get-tuple-element.37), channel_id=1, source_target_pairs={{0,1},{1,2},{2,3},{3,4},{4,5},{5,6},{6,7},{7,8},{8,9},{9,10},{10,1... | collective-permute-start | bytes 1728008 | tf_op jit(solution)/shard_map/ppermute | solution.py:29
  39.8 2.1 %collective-permute-start.2 = (bf16[1,200,1440]{2,1,0:T(8,128)(2,1)}, bf16[1,200,1440]{2,1,0:T(8,128)(2,1)}, u32[]{:S(2)}, u32[]{:S(2)}) collective-permute-start(bf16[1,200,1440]{2,1,0:T(8,128)(2,1)} %get-tuple-element.36), channel_id=1, source_target_pairs={{1,0},{2,1},{3,2},{4,3},{5,4},{6,5},{7,6},{8,7},{9,8},{10,9},{11,1... | collective-permute-start | bytes 1728008 | tf_op jit(solution)/shard_map/ppermute | solution.py:30
  41.9 0.9 fusion.50
  42.8 1.3 copy.26
  44.1 5.5 %gather_fusion = bf16[1440,200]{1,0:T(8,128)(2,1)} fusion(bf16[200,1440]{0,1:T(8,128)(2,1)S(1)} %copy.26, s32[2048]{0:T(1024)} %pad_clamp_fusion), kind=kCustom, calls=%fused_computation.2 | custom fusion | bytes 1157760 | tf_op jit(solution)/shard_map/jit(_take)/gather | solution.py:270
  49.6 2.2 %copy.27 = bf16[1440,200]{0,1:T(8,128)(2,1)} copy(bf16[1440,200]{1,0:T(8,128)(2,1)} %gather_fusion) | data formatting | bytes 1152000 | tf_op jit(solution)/shard_map/jit(_take)/gather | solution.py:270
  51.8 1.1 select_bitcast_fusion
  53.0 15.0 %collective-permute-done.1 = bf16[1,200,1440]{2,1,0:T(8,128)(2,1)S(1)} collective-permute-done((bf16[1,200,1440]{2,1,0:T(8,128)(2,1)}, bf16[1,200,1440]{2,1,0:T(8,128)(2,1)S(1)}, u32[]{:S(2)}, u32[]{:S(2)}) %collective-permute-start.1) | collective-permute-done | bytes 576032 | tf_op jit(solution)/shard_map/ppermute | solution.py:29
  67.9 1.7 %collective-permute-done.2 = bf16[1,200,1440]{2,1,0:T(8,128)(2,1)} collective-permute-done((bf16[1,200,1440]{2,1,0:T(8,128)(2,1)}, bf16[1,200,1440]{2,1,0:T(8,128)(2,1)}, u32[]{:S(2)}, u32[]{:S(2)}) %collective-permute-start.2) | collective-permute-done | bytes 576032 | tf_op jit(solution)/shard_map/ppermute | solution.py:30
  69.7 1.2 bitcast_select_fusion
  71.4 0.8 fusion.46
  72.2 0.9 fusion.48
  73.1 1.4 fusion.47
  74.6 4.8 %fusion.49 = (f32[3,200,1439]{2,1,0:T(8,128)}, f32[3,200,1439]{2,1,0:T(8,128)}) fusion(f32[3,200,1440]{2,1,0:T(8,128)S(1)} %get-tuple-element.30), kind=kLoop, calls=%fused_computation.84 | loop fusion | bytes 13814400 | tf_op jit(solution)/shard_map/jit(_roll_static)/slice | solution.py:217
  79.7 9.0 %fusion.44 = (f32[3,1440]{1,0:T(4,128)S(1)}, f32[3,200,1440]{2,1,0:T(8,128)}) fusion(f32[3,200,1]{2,1,0:T(8,128)} %get-tuple-element.26, f32[3,200,1439]{2,1,0:T(8,128)} %get-tuple-element.28, f32[200]{0:T(256)S(1)} %bitcast.67, bf16[1,200,1440]{2,1,0:T(8,128)(2,1)S(1)} %bitcast_select_fusion, bf16[3,200,1440]{2,1,0:T(8,128)(2,1)S(1)} %fusion.15, ...), kind=kLoop, calls=%fused_computation.80 | loop fusion | flops 25051680 | bytes 27096480 | tf_op jit(solution)/shard_map/reduce_sum | solution.py:41
  88.7 1.1 broadcast_in_dim.50
  89.8 7.2 %shard_map.186 = bf16[16,48,1152]{2,1,0:T(8,128)(2,1)} custom-call(bf16[16,48,1152]{2,1,0:T(8,128)(2,1)} %all-to-all-done.got_ref, bf16[768,768]{1,0:T(8,128)(2,1)} %copy.25.blocks_ref, bf16[768,768]{1,0:T(8,128)(2,1)} %bitcast.55, f32[768,384]{1,0:T(8,128)} %bitcast.56), custom_call_target="tpu_custom_call" | custom-call | flops 2717908992 | bytes 5898240 | tf_op jit(solution)/shard_map/pallas_call | solution.py:145
  97.0 4.5 %all-to-all-start.1 = ((bf16[16,48,1152]{2,1,0:T(8,128)(2,1)}), bf16[16,48,1152]{2,1,0:T(8,128)(2,1)}, u32[]{:S(2)}, u32[]{:S(2)}) async-start(bf16[16,48,1152]{2,1,0:T(8,128)(2,1)} %shard_map.186), calls=%async_computation.1 | async-start | bytes 3538944 | tf_op jit(solution)/shard_map/all_to_all | solution.py:277
  101.5 2.5 %multiply_reduce_fusion = f32[3,1440]{1,0:T(4,128)S(1)} fusion(f32[3,200,1440]{2,1,0:T(8,128)} %get-tuple-element.14, f32[3,1440]{1,0:T(4,128)S(1)} %broadcast_multiply_fusion), kind=kLoop, calls=%fused_computation.31 | loop fusion | flops 2587680 | bytes 3490560 | tf_op jit(solution)/shard_map/reduce_sum | solution.py:43
  104.1 9.0 %fusion.14 = bf16[3,200,1440]{2,1,0:T(8,128)(2,1)} fusion(f32[3,200,1440]{2,1,0:T(8,128)} %get-tuple-element.14, f32[3,1440]{1,0:T(4,128)S(1)} %copy-done.7, f32[200]{0:T(256)S(1)} %copy-done.30, f32[3,1440]{1,0:T(4,128)S(1)} %add_rsqrt_fusion, f32[3,1440]{1,0:T(4,128)S(1)} %broadcast_multiply_fusion, bf16[3,200,1440]{2,1,0:T(8,128)(2,1)S(1)} %fusion.15, ...), kind=kOutput, calls=%fused_computation.27 | convolution fusion | flops 2802816000 | bytes 7604640 | tf_op jit(solution)/shard_map/ke,rel->rkl/dot_general | solution.py:297
  113.1 0.9 slice.134
  114.0 2.3 %collective-permute-start.3 = (bf16[3,1440]{1,0:T(4,128)(2,1)S(1)}, bf16[3,1440]{1,0:T(4,128)(2,1)S(1)}, u32[]{:S(2)}, u32[]{:S(2)}) collective-permute-start(bf16[3,1440]{1,0:T(4,128)(2,1)S(1)} %bitcast.58), channel_id=1, source_target_pairs={{1,0},{2,1},{3,2},{4,3},{5,4},{6,5},{7,6},{8,7},{9,8},{10,9},{11,1... | collective-permute-start | bytes 25928 | tf_op jit(solution)/shard_map/ppermute | solution.py:22
  116.9 25.0 %collective-permute-done.3 = bf16[3,1440]{1,0:T(4,128)(2,1)S(1)} collective-permute-done((bf16[3,1440]{1,0:T(4,128)(2,1)S(1)}, bf16[3,1440]{1,0:T(4,128)(2,1)S(1)}, u32[]{:S(2)}, u32[]{:S(2)}) %collective-permute-start.3) | collective-permute-done | bytes 8672 | tf_op jit(solution)/shard_map/ppermute | solution.py:22
  143.2 10.5 %shard_map.187 = bf16[3,1440,384]{2,1,0:T(8,128)(2,1)} custom-call(bf16[768,1152]{1,0:T(8,128)(2,1)} %bitcast.4.back_ref, bf16[1440,768]{1,0:T(8,128)(2,1)} %bitcast.53, bf16[384,384]{1,0:T(8,128)(2,1)} %blend_ref.1, bf16[3,1440,384]{2,1,0:T(8,128)(2,1)} %bitcast.70, bf16[3,1,1440]{2,1,0:T(2,128)(2,1)} %broadcast_select_fusion.sst_ref, ...), custom_call_target="tpu_custom_call" | custom-call | flops 3822059520 | bytes 9437184 | tf_op jit(solution)/shard_map/pallas_call | solution.py:191
  (87 shorter events, 6.8 us)
Async XLA Ops:
  0.6 103.4 %copy-start = (bf16[200,800]{1,0:T(8,128)(2,1)S(1)}, bf16[200,800]{1,0:T(8,128)(2,1)}, u32[]{:S(2)}) copy-start(bf16[200,800]{1,0:T(8,128)(2,1)} %param.35) | copy-start | bytes 960004
  5.5 17.1 %copy-start.10 = (s32[1440]{0:T(1024)S(1)}, s32[1440]{0:T(1024)}, u32[]{:S(2)}) copy-start(s32[1440]{0:T(1024)} %param.23) | copy-start | bytes 17284
  5.5 17.7 %copy-start.11 = (s32[3,1440]{1,0:T(4,128)S(1)}, s32[3,1440]{1,0:T(4,128)}, u32[]{:S(2)}) copy-start(s32[3,1440]{1,0:T(4,128)} %param.22) | copy-start | bytes 51844
  5.5 18.3 %copy-start.12 = (f32[9,200]{1,0:T(8,128)S(1)}, f32[9,200]{1,0:T(8,128)}, u32[]{:S(2)}) copy-start(f32[9,200]{1,0:T(8,128)} %param.32) | copy-start | bytes 21604
  5.5 18.9 %copy-start.27 = (s32[3]{0:T(128)S(1)}, s32[3]{0:T(128)}, u32[]{:S(2)}) copy-start(s32[3]{0:T(128)} %param.25) | copy-start | bytes 40
  13.7 11.3 %copy-start.5 = (bf16[768,768]{0,1:T(8,128)(2,1)S(1)}, bf16[768,768]{0,1:T(8,128)(2,1)}, u32[]{:S(2)}) copy-start(bf16[768,768]{0,1:T(8,128)(2,1)} %constant.74.clone) | copy-start | bytes 3538948
  13.7 12.8 %copy-start.28 = (s32[3]{0:T(128)S(1)}, s32[3]{0:T(128)}, u32[]{:S(2)}) copy-start(s32[3]{0:T(128)} %param.24) | copy-start | bytes 40
  13.7 12.8 %copy-start.9 = (bf16[3,8,1440]{2,1,0:T(8,128)(2,1)S(1)}, bf16[3,8,1440]{2,1,0:T(8,128)(2,1)}, u32[]{:S(2)}) copy-start(bf16[3,8,1440]{2,1,0:T(8,128)(2,1)} %get-tuple-element.9) | copy-start | bytes 207364
  13.7 14.0 %copy-start.13 = (bf16[200,8]{0,1:T(8,128)(2,1)S(1)}, bf16[200,8]{0,1:T(8,128)(2,1)}, u32[]{:S(2)}) copy-start(bf16[200,8]{0,1:T(8,128)(2,1)} %param.31) | copy-start | bytes 9604
  13.7 12.8 %collective-permute-start = (bf16[3,8,1440]{2,1,0:T(8,128)(2,1)}, bf16[3,8,1440]{2,1,0:T(8,128)(2,1)S(1)}, u32[]{:S(2)}, u32[]{:S(2)}) collective-permute-start(bf16[3,8,1440]{2,1,0:T(8,128)(2,1)} %get-tuple-element.9), channel_id=1, source_target_pairs={{0,1},{1,2},{2,3},{3,4},{4,5},{5,6},{6,7},{7,8},{8,9},{9,10},{10,1... | collective-permute-start | bytes 207368 | tf_op jit(solution)/shard_map/ppermute | solution.py:22
  17.6 71.1 %all-to-all-start = ((bf16[16,48,1152]{2,1,0:T(8,128)(2,1)}), bf16[16,48,1152]{2,1,0:T(8,128)(2,1)}, u32[]{:S(2)}, u32[]{:S(2)}) async-start(bf16[16,48,1152]{2,1,0:T(8,128)(2,1)} %bitcast.54), calls=%async_computation | async-start | bytes 3538944 | tf_op jit(solution)/shard_map/all_to_all | solution.py:253
  23.2 9.2 %copy-start.6 = (f32[3,1440]{1,0:T(4,128)}, f32[3,1440]{1,0:T(4,128)S(1)}, u32[]{:S(2)}) copy-start(f32[3,1440]{1,0:T(4,128)S(1)} %convert_element_type.36) | copy-start | bytes 51844
  36.4 31.5 %collective-permute-start.1 = (bf16[1,200,1440]{2,1,0:T(8,128)(2,1)}, bf16[1,200,1440]{2,1,0:T(8,128)(2,1)S(1)}, u32[]{:S(2)}, u32[]{:S(2)}) collective-permute-start(bf16[1,200,1440]{2,1,0:T(8,128)(2,1)} %get-tuple-element.37), channel_id=1, source_target_pairs={{0,1},{1,2},{2,3},{3,4},{4,5},{5,6},{6,7},{7,8},{8,9},{9,10},{10,1... | collective-permute-start | bytes 1728008 | tf_op jit(solution)/shard_map/ppermute | solution.py:29
  39.8 29.9 %collective-permute-start.2 = (bf16[1,200,1440]{2,1,0:T(8,128)(2,1)}, bf16[1,200,1440]{2,1,0:T(8,128)(2,1)}, u32[]{:S(2)}, u32[]{:S(2)}) collective-permute-start(bf16[1,200,1440]{2,1,0:T(8,128)(2,1)} %get-tuple-element.36), channel_id=1, source_target_pairs={{1,0},{2,1},{3,2},{4,3},{5,4},{6,5},{7,6},{8,7},{9,8},{10,9},{11,1... | collective-permute-start | bytes 1728008 | tf_op jit(solution)/shard_map/ppermute | solution.py:30
  74.5 5.1 %copy-start.4 = (f32[3,200,1]{2,1,0:T(8,128)S(1)}, f32[3,200,1]{2,1,0:T(8,128)}, u32[]{:S(2)}) copy-start(f32[3,200,1]{2,1,0:T(8,128)} %get-tuple-element.32) | copy-start | bytes 7204
  74.5 5.1 %copy-start.14 = (f32[1,200]{1,0:T(1,128)S(1)}, f32[1,200]{1,0:T(1,128)}, u32[]{:S(2)}) copy-start(f32[1,200]{1,0:T(1,128)} %get-tuple-element.38) | copy-start | bytes 2404
  74.5 5.1 %copy-start.15 = (f32[1,200]{1,0:T(1,128)S(1)}, f32[1,200]{1,0:T(1,128)}, u32[]{:S(2)}) copy-start(f32[1,200]{1,0:T(1,128)} %get-tuple-element.39) | copy-start | bytes 2404
  74.5 5.1 %copy-start.16 = (f32[1,200]{1,0:T(1,128)S(1)}, f32[1,200]{1,0:T(1,128)}, u32[]{:S(2)}) copy-start(f32[1,200]{1,0:T(1,128)} %get-tuple-element.40) | copy-start | bytes 2404
  74.5 5.1 %copy-start.17 = (f32[1,200]{1,0:T(1,128)S(1)}, f32[1,200]{1,0:T(1,128)}, u32[]{:S(2)}) copy-start(f32[1,200]{1,0:T(1,128)} %get-tuple-element.41) | copy-start | bytes 2404
  74.6 5.1 %copy-start.18 = (f32[1,200]{1,0:T(1,128)S(1)}, f32[1,200]{1,0:T(1,128)}, u32[]{:S(2)}) copy-start(f32[1,200]{1,0:T(1,128)} %get-tuple-element.42) | copy-start | bytes 2404
  74.6 5.1 %copy-start.19 = (f32[1,200]{1,0:T(1,128)S(1)}, f32[1,200]{1,0:T(1,128)}, u32[]{:S(2)}) copy-start(f32[1,200]{1,0:T(1,128)} %get-tuple-element.43) | copy-start | bytes 2404
  74.6 5.1 %copy-start.20 = (f32[1,200]{1,0:T(1,128)S(1)}, f32[1,200]{1,0:T(1,128)}, u32[]{:S(2)}) copy-start(f32[1,200]{1,0:T(1,128)} %get-tuple-element.44) | copy-start | bytes 2404
  74.6 5.1 %copy-start.21 = (f32[1,200]{1,0:T(1,128)S(1)}, f32[1,200]{1,0:T(1,128)}, u32[]{:S(2)}) copy-start(f32[1,200]{1,0:T(1,128)} %get-tuple-element.45) | copy-start | bytes 2404
  79.7 9.0 %copy-start.8 = (f32[48,384]{1,0:T(8,128)S(1)}, f32[48,384]{1,0:T(8,128)}, u32[]{:S(2)}) copy-start(f32[48,384]{1,0:T(8,128)} %param.27) | copy-start | bytes 221188
  97.0 7.0 %copy-start.7 = (f32[3,1440]{1,0:T(4,128)S(1)}, f32[3,1440]{1,0:T(4,128)}, u32[]{:S(2)}) copy-start(f32[3,1440]{1,0:T(4,128)} %copy-done.6) | copy-start | bytes 51844
  97.0 7.0 %copy-start.29 = (bf16[800,200]{0,1:T(8,128)(2,1)S(1)}, bf16[800,200]{0,1:T(8,128)(2,1)}, u32[]{:S(2)}) copy-start(bf16[800,200]{0,1:T(8,128)(2,1)} %param.34) | copy-start | bytes 960004
  97.0 7.1 %copy-start.30 = (f32[200]{0:T(256)S(1)}, f32[200]{0:T(256)}, u32[]{:S(2)}) copy-start(f32[200]{0:T(256)} %param.33) | copy-start | bytes 2404
  97.0 46.2 %all-to-all-start.1 = ((bf16[16,48,1152]{2,1,0:T(8,128)(2,1)}), bf16[16,48,1152]{2,1,0:T(8,128)(2,1)}, u32[]{:S(2)}, u32[]{:S(2)}) async-start(bf16[16,48,1152]{2,1,0:T(8,128)(2,1)} %shard_map.186), calls=%async_computation.1 | async-start | bytes 3538944 | tf_op jit(solution)/shard_map/all_to_all | solution.py:277
  104.0 12.3 %copy-start.26 = (s32[3]{0:T(128)S(1)}, s32[3]{0:T(128)}, u32[]{:S(2)}) copy-start(s32[3]{0:T(128)} %get-tuple-element.20) | copy-start | bytes 40
  104.0 12.3 %copy-start.25 = (f32[384]{0:T(512)S(1)}, f32[384]{0:T(512)}, u32[]{:S(2)}) copy-start(f32[384]{0:T(512)} %param.30) | copy-start | bytes 4612
  104.0 38.5 %copy-start.23 = (pred[3]{0:T(512)(128)(4,1)S(1)}, pred[3]{0:T(512)(128)(4,1)}, u32[]{:S(2)}) copy-start(pred[3]{0:T(512)(128)(4,1)} %get-tuple-element.19) | copy-start | bytes 13
  114.0 28.0 %collective-permute-start.3 = (bf16[3,1440]{1,0:T(4,128)(2,1)S(1)}, bf16[3,1440]{1,0:T(4,128)(2,1)S(1)}, u32[]{:S(2)}, u32[]{:S(2)}) collective-permute-start(bf16[3,1440]{1,0:T(4,128)(2,1)S(1)} %bitcast.58), channel_id=1, source_target_pairs={{1,0},{2,1},{3,2},{4,3},{5,4},{6,5},{7,6},{8,7},{9,8},{10,9},{11,1... | collective-permute-start | bytes 25928 | tf_op jit(solution)/shard_map/ppermute | solution.py:22
  (5 other events, 24.3 us)
